TPU v7x, 256 devices: a whole 4x4x8 slice. The times are simulated.
256 devices in a mesh: ctx: 32 (over x, z), pb: 2 (over core), ga: 4 (over y).
Axes of the slice: x: 4, y: 4, z: 8, core: 2. Of those that a mesh axis runs over, the one named last changes fastest.
Arguments:
- queries: bfloat16 [8192, 12288], P(('ctx', 'pb'), 'ga'), may hold values from -128 to 128
- stretch_keys: bfloat16 [8192, 768], P(('ctx', 'pb'), 'ga'), may hold values from -16 to 16
- stretch_values: bfloat16 [8192, 512], P(('ctx', 'pb'), 'ga'), may hold values from -6 to 6
- prior_cache_keys: bfloat16 [131072, 768], P('ctx', 'ga'), may hold values from -16 to 16
- cache_values: bfloat16 [131072, 512], P('ctx', 'ga'), may hold values from -6 to 6
- block_lengths: int32 [32, 256], P('ctx'), may hold values from 1 to 32, 4096 in all within a row
- compress_weights: float32 [4, 32], P('ga'), may hold values from 0.1 to 1.9
- selections: int32 [128, 4, 13], P(('ctx', 'pb'), 'ga'), may hold values from 1 to 2045, as said below
- gate_logits: float32 [3, 8192, 64], P(None, ('ctx', 'pb'), 'ga'), may hold values from -6 to 6
Outputs:
- attended: bfloat16 [8192, 8192], P(('ctx', 'pb'), 'ga')
Inputs may be any that keep to these rules, and one draw needn't show every extreme that they name: `block_lengths`: each row belongs to one cache shard and sums to 4096; its largest entry is 32. `selections`: each row lists 13 different blocks, never the first or one of the last two blocks of a cache shard (a shard holds 64 blocks). Over the 2 rows of one device and one group at most 2 listed blocks lie in one cache shard, and for each group one cache shard holds exactly 2 of every device's listed blocks.
All inputs are finite; a program needn't handle non-finite values.
Results may differ from a plain program's by a relative error of at most 0.011.
Values may be sent and summed in bfloat16 or wider, within the bound.
A program may use at most 128 MiB of HBM per device.

v0:
```python
import math
import jax
import jax.numpy as jnp
from jax import lax
from jax.sharding import PartitionSpec as P

SBLK = 64
WINDOW = 512
floor_score = -1e30


def passed_along(value, axis, steps):
    count = lax.axis_size(axis)
    first, last = (max(0, -steps), min(count, count - steps))
    return lax.ppermute(value, axis, [(source, source + steps) for source in range(first, last)])


def compress_rows(cache_rows, value_rows, lengths, branch_weights):
    span = cache_rows.shape[0]
    starts = jnp.cumsum(lengths) - lengths
    positions = jnp.arange(span, dtype=jnp.int32)
    group_member = (positions[None, :] >= starts[:, None]) & (
        positions[None, :] < (starts + lengths)[:, None]
    )
    offsets = jnp.sum(jnp.where(group_member, positions[None, :] - starts[:, None], 0), axis=0)
    lookup = jnp.arange(branch_weights.shape[0], dtype=jnp.int32)
    token_weight = jnp.sum(
        jnp.where(offsets[:, None] == lookup[None, :], branch_weights[None, :], 0.0), axis=1
    )
    spread = 1.0 / jnp.sqrt(lengths.astype(jnp.float32))
    matrix = jnp.where(group_member, token_weight[None, :] * spread[:, None], 0.0).astype(
        jnp.bfloat16
    )
    packed_keys = jnp.dot(matrix, cache_rows, preferred_element_type=jnp.float32).astype(
        jnp.bfloat16
    )
    packed_values = jnp.dot(matrix, value_rows, preferred_element_type=jnp.float32).astype(
        jnp.bfloat16
    )
    return (packed_keys, packed_values)


def wanted_blocks(listed_ids, block_total):
    flat_ids = listed_ids.reshape(-1)
    always_on = jnp.array([0, block_total - 2, block_total - 1], dtype=jnp.int32)
    flat_ids = jnp.concatenate([always_on, flat_ids])
    return flat_ids


def slot_table(flat_ids, per_shard, slot_width):
    owners = flat_ids // per_shard
    position = jnp.arange(flat_ids.shape[0], dtype=jnp.int32)
    before = (owners[None, :] == owners[:, None]) & (position[None, :] < position[:, None])
    rank_count = jnp.sum(before.astype(jnp.int32), axis=1)
    return (owners * slot_width + rank_count, flat_ids % per_shard)


def asked_table(slots, offsets, shards, slot_width):
    places = jnp.arange(shards * slot_width, dtype=jnp.int32)
    matches = slots[:, None] == places[None, :]
    full_table = jnp.sum(jnp.where(matches, offsets[:, None], 0), axis=0)
    return full_table.reshape(shards, slot_width)


def on_device(
    queries,
    stretch_keys,
    stretch_values,
    prior_cache_keys,
    cache_values,
    block_lengths,
    compress_weights,
    selections,
    gate_logits,
):
    query_count = queries.shape[0]
    head_count = gate_logits.shape[2]
    key_width = prior_cache_keys.shape[1]
    value_width = cache_values.shape[1]
    score_scale = 1.0 / math.sqrt(key_width)
    query_rows = queries.reshape(query_count * head_count, key_width)
    row_count = query_rows.shape[0]
    shards = lax.axis_size("ctx")
    packed_keys, packed_values = compress_rows(
        prior_cache_keys, cache_values, block_lengths[0], compress_weights[0]
    )
    start_state = (
        jnp.full((row_count,), floor_score, jnp.float32),
        jnp.zeros((row_count,), jnp.float32),
        jnp.zeros((row_count, value_width), jnp.float32),
    )
    piece_keys = lax.all_gather(packed_keys, "ctx", axis=0, tiled=True)
    piece_values = lax.all_gather(packed_values, "ctx", axis=0, tiled=True)
    length = piece_keys.shape[0]
    stride = math.gcd(length, 1024)
    key_block = piece_keys.reshape(length // stride, stride, key_width)
    value_block = piece_values.reshape(length // stride, stride, value_width)

    def absorb(carry_state, operand):
        row_peak, running_total, blended = carry_state
        some_keys, some_values = operand
        scores = (
            lax.dot_general(
                query_rows, some_keys, (((1,), (1,)), ((), ())), preferred_element_type=jnp.float32
            )
            * score_scale
        )
        new_peak = jnp.maximum(row_peak, jnp.max(scores, axis=1))
        factor = jnp.exp(row_peak - new_peak)
        branch_weights = jnp.exp(scores - new_peak[:, None])
        running_total = running_total * factor + jnp.sum(branch_weights, axis=1)
        blended = blended * factor[:, None] + jnp.dot(
            branch_weights.astype(jnp.bfloat16), some_values, preferred_element_type=jnp.float32
        )
        return ((new_peak, running_total, blended), None)

    row_peak, running_total, blended = lax.scan(absorb, start_state, (key_block, value_block))[0]
    compressed_out = (blended / running_total[:, None]).reshape(
        query_count, head_count, value_width
    )
    listed_ids = selections[:, 0, :]
    query_blocks, listed = listed_ids.shape
    per_shard = prior_cache_keys.shape[0] // SBLK
    block_total = per_shard * shards
    slot_bound = max(2, (query_blocks * listed + shards - 1) // shards)
    key_blocks = prior_cache_keys.reshape(per_shard, SBLK, key_width)
    value_blocks = cache_values.reshape(per_shard, SBLK, value_width)
    slot_width = slot_bound + 2
    slots, offsets = slot_table(wanted_blocks(listed_ids, block_total), per_shard, slot_width)
    asked_here = asked_table(slots, offsets, shards, slot_width)
    asked_for = lax.all_to_all(asked_here, "ctx", split_axis=0, concat_axis=0, tiled=True)
    item_count = asked_for.shape[1]
    flat_asked = asked_for.reshape(-1)
    sent_keys = jnp.take(key_blocks, flat_asked, axis=0).reshape(
        shards, item_count, SBLK, key_width
    )
    sent_values = jnp.take(value_blocks, flat_asked, axis=0).reshape(
        shards, item_count, SBLK, value_width
    )
    got_keys = lax.all_to_all(sent_keys, "ctx", split_axis=0, concat_axis=0, tiled=True)
    got_values = lax.all_to_all(sent_values, "ctx", split_axis=0, concat_axis=0, tiled=True)
    picked_keys = jnp.take(got_keys.reshape(shards * slot_width, SBLK, key_width), slots, axis=0)
    picked_values = jnp.take(
        got_values.reshape(shards * slot_width, SBLK, value_width), slots, axis=0
    )
    fixed_keys = picked_keys[:3]
    fixed_values = picked_values[:3]
    listed_keys = picked_keys[3:]
    listed_values = picked_values[3:]
    selected_keys = jnp.concatenate(
        [
            jnp.broadcast_to(fixed_keys[None], (query_blocks, 3, SBLK, key_width)),
            listed_keys.reshape(query_blocks, listed, SBLK, key_width),
        ],
        axis=1,
    ).reshape(query_blocks, (3 + listed) * SBLK, key_width)
    chosen_values = jnp.concatenate(
        [
            jnp.broadcast_to(fixed_values[None], (query_blocks, 3, SBLK, value_width)),
            listed_values.reshape(query_blocks, listed, SBLK, value_width),
        ],
        axis=1,
    ).reshape(query_blocks, (3 + listed) * SBLK, value_width)
    grouped_rows = queries.reshape(query_blocks, query_count // query_blocks, head_count, key_width)
    scores = (
        jnp.einsum(
            "rjve,rse->rjvs", grouped_rows, selected_keys, preferred_element_type=jnp.float32
        )
        * score_scale
    )
    row_peak = jnp.max(scores, axis=3, keepdims=True)
    branch_weights = jnp.exp(scores - row_peak)
    row_total = jnp.sum(branch_weights, axis=3, keepdims=True)
    selected_out = (
        jnp.einsum(
            "bqhk,bkv->bqhv",
            branch_weights.astype(jnp.bfloat16),
            chosen_values,
            preferred_element_type=jnp.float32,
        )
        / row_total
    )
    selected_out = selected_out.reshape(query_count, head_count, value_width)
    reach_count = max(1, WINDOW // query_count)
    earlier_keys = []
    earlier_values = []
    for distance in range(reach_count, 0, -1):
        moved_keys, moved_values = passed_along(
            (stretch_keys, stretch_values), ("ctx", "pb"), distance
        )
        earlier_keys.append(moved_keys)
        earlier_values.append(moved_values)
    window_rows = jnp.concatenate(earlier_keys + [stretch_keys], axis=0)
    window_values = jnp.concatenate(earlier_values + [stretch_values], axis=0)
    first_query = lax.axis_index(("ctx", "pb")) * query_count
    query_pos = first_query + jnp.arange(query_count, dtype=jnp.int32)
    key_pos = (
        first_query - reach_count * query_count + jnp.arange(window_rows.shape[0], dtype=jnp.int32)
    )
    distance_grid = query_pos[:, None] - key_pos[None, :]
    allowed = (distance_grid >= 0) & (distance_grid < WINDOW) & (key_pos[None, :] >= 0)
    near_scores = (
        jnp.einsum(
            "qhd,kd->qhk",
            queries.reshape(query_count, head_count, key_width),
            window_rows,
            preferred_element_type=jnp.float32,
        )
        * score_scale
    )
    near_scores = jnp.where(allowed[:, None, :], near_scores, floor_score)
    near_peak = jnp.max(near_scores, axis=2, keepdims=True)
    near_weights = jnp.exp(near_scores - near_peak)
    near_total = jnp.sum(near_weights, axis=2, keepdims=True)
    windowed_out = (
        jnp.einsum(
            "qhk,kv->qhv",
            near_weights.astype(jnp.bfloat16),
            window_values,
            preferred_element_type=jnp.float32,
        )
        / near_total
    )
    gate_values = jax.nn.sigmoid(gate_logits)
    attended = (
        gate_values[0][..., None] * compressed_out
        + gate_values[1][..., None] * selected_out
        + gate_values[2][..., None] * windowed_out
    )
    return attended.reshape(query_count, head_count * value_width).astype(jnp.bfloat16)


def solution(mesh):
    placed = (
        P(("ctx", "pb"), "ga"),
        P(("ctx", "pb"), "ga"),
        P(("ctx", "pb"), "ga"),
        P("ctx", "ga"),
        P("ctx", "ga"),
        P("ctx", None),
        P("ga", None),
        P(("ctx", "pb"), "ga", None),
        P(None, ("ctx", "pb"), "ga"),
    )
    return jax.shard_map(
        on_device, mesh=mesh, in_specs=placed, out_specs=P(("ctx", "pb"), "ga"), check_vma=False
    )
```

profile of v0, /device:TPU:24, one launch (start us, length us, event | category | flops | bytes accessed | tf_op | source)
XLA Modules:
  0.0 363.3 jit_solution(14902906855570495999)
XLA Ops:
  17.9 11.3 %all-to-all-start = ((s32[32,1,4]{2,1,0:T(1,128)}), s32[32,1,4]{2,1,0:T(1,128)S(1)}, u32[]{:S(2)}, u32[]{:S(2)}) async-start(s32[32,1,4]{2,1,0:T(1,128)} %bitcast.9), calls=%async_computation | async-start | bytes 32768 | tf_op jit(solution)/shard_map/all_to_all | solution.py:131
  49.8 9.3 %all-to-all-start.2 = ((bf16[32,4,64,128]{3,2,1,0:T(8,128)(2,1)}), bf16[32,4,64,128]{3,2,1,0:T(8,128)(2,1)}, u32[]{:S(2)}, u32[]{:S(2)}) async-start(bf16[32,4,64,128]{3,2,1,0:T(8,128)(2,1)} %broadcast_select_fusion.1), calls=%async_computation.2 | async-start | bytes 4194304 | tf_op jit(solution)/shard_map/all_to_all | solution.py:141
  82.3 30.3 %collective-permute-done.5 = bf16[128,128]{0,1:T(8,128)(2,1)S(1)} collective-permute-done((bf16[128,128]{0,1:T(8,128)(2,1)S(1)}, bf16[128,128]{0,1:T(8,128)(2,1)S(1)}, u32[]{:S(2)}, u32[]{:S(2)}) %collective-permute-start.5) | collective-permute-done | bytes 32800 | tf_op jit(solution)/shard_map/ppermute | solution.py:15
  112.5 6.4 %collective-permute-start.6 = (bf16[128,128]{0,1:T(8,128)(2,1)S(1)}, bf16[128,128]{0,1:T(8,128)(2,1)S(1)}, u32[]{:S(2)}, u32[]{:S(2)}) collective-permute-start(bf16[128,128]{0,1:T(8,128)(2,1)S(1)} %copy.92), channel_id=1, source_target_pairs={{0,8},{4,12},{8,16},{12,20},{16,24},{20,28},{24,32},{28,36},{32,40... | collective-permute-start | bytes 98312 | tf_op jit(solution)/shard_map/ppermute | solution.py:15
  128.1 17.3 %all-to-all-start.1 = ((bf16[32,4,64,192]{3,2,1,0:T(8,128)(2,1)}), bf16[32,4,64,192]{3,2,1,0:T(8,128)(2,1)}, u32[]{:S(2)}, u32[]{:S(2)}) async-start(bf16[32,4,64,192]{3,2,1,0:T(8,128)(2,1)} %broadcast_select_fusion), calls=%async_computation.1 | async-start | bytes 8388608 | tf_op jit(solution)/shard_map/all_to_all | solution.py:140
  148.7 6.0 %copy.102 = bf16[8192,192]{1,0:T(8,128)(2,1)} copy(bf16[8192,192]{0,1:T(8,128)(2,1)} %all-gather.3.cloned.1.call-done) | data formatting | bytes 6291456
  154.6 69.5 %all-gather.5.cloned.1.call-done = bf16[8192,128]{1,0:T(8,128)(2,1)} async-done(((bf16[256,128]{1,0:T(8,128)(2,1)}), bf16[8192,128]{1,0:T(8,128)(2,1)}) %all-gather.5.cloned.1.call-update) | async-done | bytes 2097168 | tf_op jit(solution)/shard_map/all_gather | solution.py:93
  224.1 114.3 %while.15 = (s32[]{:T(128)}, f32[2048]{0:T(1024)S(1)}, f32[2048]{0:T(1024)S(1)}, f32[2048,128]{1,0:T(8,128)S(1)}, bf16[8,1024,192]{2,1,0:T(8,128)(2,1)}, /*index...) while((s32[]{:T(128)}, f32[2048]{0:T(1024)S(1)}, ...), condition=%wide.region_7.8_spmd.clone, body=%wide.region_4.7_spmd.clone.sunk | while | flops 1359751168 | bytes 62522500 | solution.py:117
  224.1 5.5 %multiply_reduce_fusion.2 = (f32[2048]{0:T(1024)S(1)}, f32[1024,2048]{1,0:T(8,128)}) fusion(bf16[2048,192]{1,0:T(8,128)(2,1)S(1)} %get-tuple-element.209, bf16[8,1024,192]{2,1,0:T(8,128)(2,1)} %get-tuple-element.208, s32[]{:T(128)} %get-tuple-element.195), kind=kOutput, calls=%fused_computation.5.clone.1 | convolution fusion | flops 809498624 | bytes 9708032 | tf_op jit(solution)/shard_map/while/body/eval_jaxpr/dot_general | solution.py:103
  229.7 4.9 %fusion.72 = f32[2048]{0:T(1024)S(1)} fusion(f32[1024,2048]{1,0:T(8,128)} %get-tuple-element.183, f32[2048]{0:T(1024)S(1)} %select_maximum_fusion.2), kind=kLoop, calls=%fused_computation.7.clone.1 | loop fusion | flops 6289408 | bytes 8404992 | tf_op jit(solution)/shard_map/while/body/eval_jaxpr/reduce_sum | solution.py:111
  238.4 5.6 %multiply_reduce_fusion.2 = (f32[2048]{0:T(1024)S(1)}, f32[1024,2048]{1,0:T(8,128)}) fusion(bf16[2048,192]{1,0:T(8,128)(2,1)S(1)} %get-tuple-element.209, bf16[8,1024,192]{2,1,0:T(8,128)(2,1)} %get-tuple-element.208, s32[]{:T(128)} %get-tuple-element.195), kind=kOutput, calls=%fused_computation.5.clone.1 | convolution fusion | flops 809498624 | bytes 9708032 | tf_op jit(solution)/shard_map/while/body/eval_jaxpr/dot_general | solution.py:103
  244.0 4.9 %fusion.72 = f32[2048]{0:T(1024)S(1)} fusion(f32[1024,2048]{1,0:T(8,128)} %get-tuple-element.183, f32[2048]{0:T(1024)S(1)} %select_maximum_fusion.2), kind=kLoop, calls=%fused_computation.7.clone.1 | loop fusion | flops 6289408 | bytes 8404992 | tf_op jit(solution)/shard_map/while/body/eval_jaxpr/reduce_sum | solution.py:111
  252.7 5.6 %multiply_reduce_fusion.2 = (f32[2048]{0:T(1024)S(1)}, f32[1024,2048]{1,0:T(8,128)}) fusion(bf16[2048,192]{1,0:T(8,128)(2,1)S(1)} %get-tuple-element.209, bf16[8,1024,192]{2,1,0:T(8,128)(2,1)} %get-tuple-element.208, s32[]{:T(128)} %get-tuple-element.195), kind=kOutput, calls=%fused_computation.5.clone.1 | convolution fusion | flops 809498624 | bytes 9708032 | tf_op jit(solution)/shard_map/while/body/eval_jaxpr/dot_general | solution.py:103
  258.3 4.9 %fusion.72 = f32[2048]{0:T(1024)S(1)} fusion(f32[1024,2048]{1,0:T(8,128)} %get-tuple-element.183, f32[2048]{0:T(1024)S(1)} %select_maximum_fusion.2), kind=kLoop, calls=%fused_computation.7.clone.1 | loop fusion | flops 6289408 | bytes 8404992 | tf_op jit(solution)/shard_map/while/body/eval_jaxpr/reduce_sum | solution.py:111
  267.0 5.6 %multiply_reduce_fusion.2 = (f32[2048]{0:T(1024)S(1)}, f32[1024,2048]{1,0:T(8,128)}) fusion(bf16[2048,192]{1,0:T(8,128)(2,1)S(1)} %get-tuple-element.209, bf16[8,1024,192]{2,1,0:T(8,128)(2,1)} %get-tuple-element.208, s32[]{:T(128)} %get-tuple-element.195), kind=kOutput, calls=%fused_computation.5.clone.1 | convolution fusion | flops 809498624 | bytes 9708032 | tf_op jit(solution)/shard_map/while/body/eval_jaxpr/dot_general | solution.py:103
  272.6 4.9 %fusion.72 = f32[2048]{0:T(1024)S(1)} fusion(f32[1024,2048]{1,0:T(8,128)} %get-tuple-element.183, f32[2048]{0:T(1024)S(1)} %select_maximum_fusion.2), kind=kLoop, calls=%fused_computation.7.clone.1 | loop fusion | flops 6289408 | bytes 8404992 | tf_op jit(solution)/shard_map/while/body/eval_jaxpr/reduce_sum | solution.py:111
  281.3 5.6 %multiply_reduce_fusion.2 = (f32[2048]{0:T(1024)S(1)}, f32[1024,2048]{1,0:T(8,128)}) fusion(bf16[2048,192]{1,0:T(8,128)(2,1)S(1)} %get-tuple-element.209, bf16[8,1024,192]{2,1,0:T(8,128)(2,1)} %get-tuple-element.208, s32[]{:T(128)} %get-tuple-element.195), kind=kOutput, calls=%fused_computation.5.clone.1 | convolution fusion | flops 809498624 | bytes 9708032 | tf_op jit(solution)/shard_map/while/body/eval_jaxpr/dot_general | solution.py:103
  286.8 4.9 %fusion.72 = f32[2048]{0:T(1024)S(1)} fusion(f32[1024,2048]{1,0:T(8,128)} %get-tuple-element.183, f32[2048]{0:T(1024)S(1)} %select_maximum_fusion.2), kind=kLoop, calls=%fused_computation.7.clone.1 | loop fusion | flops 6289408 | bytes 8404992 | tf_op jit(solution)/shard_map/while/body/eval_jaxpr/reduce_sum | solution.py:111
  295.6 5.6 %multiply_reduce_fusion.2 = (f32[2048]{0:T(1024)S(1)}, f32[1024,2048]{1,0:T(8,128)}) fusion(bf16[2048,192]{1,0:T(8,128)(2,1)S(1)} %get-tuple-element.209, bf16[8,1024,192]{2,1,0:T(8,128)(2,1)} %get-tuple-element.208, s32[]{:T(128)} %get-tuple-element.195), kind=kOutput, calls=%fused_computation.5.clone.1 | convolution fusion | flops 809498624 | bytes 9708032 | tf_op jit(solution)/shard_map/while/body/eval_jaxpr/dot_general | solution.py:103
  301.1 4.9 %fusion.72 = f32[2048]{0:T(1024)S(1)} fusion(f32[1024,2048]{1,0:T(8,128)} %get-tuple-element.183, f32[2048]{0:T(1024)S(1)} %select_maximum_fusion.2), kind=kLoop, calls=%fused_computation.7.clone.1 | loop fusion | flops 6289408 | bytes 8404992 | tf_op jit(solution)/shard_map/while/body/eval_jaxpr/reduce_sum | solution.py:111
  309.9 5.6 %multiply_reduce_fusion.2 = (f32[2048]{0:T(1024)S(1)}, f32[1024,2048]{1,0:T(8,128)}) fusion(bf16[2048,192]{1,0:T(8,128)(2,1)S(1)} %get-tuple-element.209, bf16[8,1024,192]{2,1,0:T(8,128)(2,1)} %get-tuple-element.208, s32[]{:T(128)} %get-tuple-element.195), kind=kOutput, calls=%fused_computation.5.clone.1 | convolution fusion | flops 809498624 | bytes 9708032 | tf_op jit(solution)/shard_map/while/body/eval_jaxpr/dot_general | solution.py:103
  315.4 4.9 %fusion.72 = f32[2048]{0:T(1024)S(1)} fusion(f32[1024,2048]{1,0:T(8,128)} %get-tuple-element.183, f32[2048]{0:T(1024)S(1)} %select_maximum_fusion.2), kind=kLoop, calls=%fused_computation.7.clone.1 | loop fusion | flops 6289408 | bytes 8404992 | tf_op jit(solution)/shard_map/while/body/eval_jaxpr/reduce_sum | solution.py:111
  324.2 5.6 %multiply_reduce_fusion.2 = (f32[2048]{0:T(1024)S(1)}, f32[1024,2048]{1,0:T(8,128)}) fusion(bf16[2048,192]{1,0:T(8,128)(2,1)S(1)} %get-tuple-element.209, bf16[8,1024,192]{2,1,0:T(8,128)(2,1)} %get-tuple-element.208, s32[]{:T(128)} %get-tuple-element.195), kind=kOutput, calls=%fused_computation.5.clone.1 | convolution fusion | flops 809498624 | bytes 9708032 | tf_op jit(solution)/shard_map/while/body/eval_jaxpr/dot_general | solution.py:103
  329.7 4.9 %fusion.72 = f32[2048]{0:T(1024)S(1)} fusion(f32[1024,2048]{1,0:T(8,128)} %get-tuple-element.183, f32[2048]{0:T(1024)S(1)} %select_maximum_fusion.2), kind=kLoop, calls=%fused_computation.7.clone.1 | loop fusion | flops 6289408 | bytes 8404992 | tf_op jit(solution)/shard_map/while/body/eval_jaxpr/reduce_sum | solution.py:111
  (188 shorter events, 115.0 us)
Async XLA Ops:
  6.5 40.7 %copy-start = (bf16[4096,128]{1,0:T(8,128)(2,1)S(1)}, bf16[4096,128]{1,0:T(8,128)(2,1)}, u32[]{:S(2)}) copy-start(bf16[4096,128]{1,0:T(8,128)(2,1)} %param.16) | copy-start | bytes 3145732
  6.5 142.1 %all-gather.3.cloned.1.call-start = ((), (), s32[]{:S(2)}) async-start(), calls=%async_computation.3 | async-start | bytes 3244032 | tf_op jit(solution)/shard_map/all_gather | solution.py:92
  11.5 17.7 %copy-start.8 = (bf16[128,192]{0,1:T(8,128)(2,1)S(1)}, bf16[128,192]{0,1:T(8,128)(2,1)}, u32[]{:S(2)}) copy-start(bf16[128,192]{0,1:T(8,128)(2,1)} %param.13) | copy-start | bytes 147460
  11.5 32.0 %copy-start.9 = (bf16[128,128]{1,0:T(8,128)(2,1)S(1)}, bf16[128,128]{1,0:T(8,128)(2,1)}, u32[]{:S(2)}) copy-start(bf16[128,128]{1,0:T(8,128)(2,1)} %param.14) | copy-start | bytes 98308
  17.9 28.3 %all-to-all-start = ((s32[32,1,4]{2,1,0:T(1,128)}), s32[32,1,4]{2,1,0:T(1,128)S(1)}, u32[]{:S(2)}, u32[]{:S(2)}) async-start(s32[32,1,4]{2,1,0:T(1,128)} %bitcast.9), calls=%async_computation | async-start | bytes 32768 | tf_op jit(solution)/shard_map/all_to_all | solution.py:131
  29.2 94.3 %collective-permute-start = (bf16[128,192]{0,1:T(8,128)(2,1)S(1)}, bf16[128,192]{0,1:T(8,128)(2,1)S(1)}, u32[]{:S(2)}, u32[]{:S(2)}) collective-permute-start(bf16[128,192]{0,1:T(8,128)(2,1)S(1)} %copy-done.8), channel_id=1, source_target_pairs={{0,16},{4,20},{8,24},{12,28},{16,32},{20,36},{24,40},{28,44},{32,4... | collective-permute-start | bytes 147464 | tf_op jit(solution)/shard_map/ppermute | solution.py:15
  33.8 89.7 %collective-permute-start.1 = (bf16[128,192]{0,1:T(8,128)(2,1)S(1)}, bf16[128,192]{0,1:T(8,128)(2,1)S(1)}, u32[]{:S(2)}, u32[]{:S(2)}) collective-permute-start(bf16[128,192]{0,1:T(8,128)(2,1)S(1)} %copy-done.8), channel_id=1, source_target_pairs={{0,12},{4,16},{8,20},{12,24},{16,28},{20,32},{24,36},{28,40},{32,4... | collective-permute-start | bytes 147464 | tf_op jit(solution)/shard_map/ppermute | solution.py:15
  35.8 87.7 %collective-permute-start.2 = (bf16[128,192]{0,1:T(8,128)(2,1)S(1)}, bf16[128,192]{0,1:T(8,128)(2,1)S(1)}, u32[]{:S(2)}, u32[]{:S(2)}) collective-permute-start(bf16[128,192]{0,1:T(8,128)(2,1)S(1)} %copy-done.8), channel_id=1, source_target_pairs={{0,8},{4,12},{8,16},{12,20},{16,24},{20,28},{24,32},{28,36},{32,40... | collective-permute-start | bytes 147464 | tf_op jit(solution)/shard_map/ppermute | solution.py:15
  40.4 83.2 %collective-permute-start.3 = (bf16[128,192]{0,1:T(8,128)(2,1)S(1)}, bf16[128,192]{0,1:T(8,128)(2,1)S(1)}, u32[]{:S(2)}, u32[]{:S(2)}) collective-permute-start(bf16[128,192]{0,1:T(8,128)(2,1)S(1)} %copy-done.8), channel_id=1, source_target_pairs={{0,4},{4,8},{8,12},{12,16},{16,20},{20,24},{24,28},{28,32},{32,36}... | collective-permute-start | bytes 147464 | tf_op jit(solution)/shard_map/ppermute | solution.py:15
  43.6 36.1 %collective-permute-start.4 = (bf16[128,128]{0,1:T(8,128)(2,1)S(1)}, bf16[128,128]{0,1:T(8,128)(2,1)S(1)}, u32[]{:S(2)}, u32[]{:S(2)}) collective-permute-start(bf16[128,128]{0,1:T(8,128)(2,1)S(1)} %copy.92), channel_id=1, source_target_pairs={{0,16},{4,20},{8,24},{12,28},{16,32},{20,36},{24,40},{28,44},{32,4... | collective-permute-start | bytes 98312 | tf_op jit(solution)/shard_map/ppermute | solution.py:15
  49.8 78.2 %all-to-all-start.2 = ((bf16[32,4,64,128]{3,2,1,0:T(8,128)(2,1)}), bf16[32,4,64,128]{3,2,1,0:T(8,128)(2,1)}, u32[]{:S(2)}, u32[]{:S(2)}) async-start(bf16[32,4,64,128]{3,2,1,0:T(8,128)(2,1)} %broadcast_select_fusion.1), calls=%async_computation.2 | async-start | bytes 4194304 | tf_op jit(solution)/shard_map/all_to_all | solution.py:141
  59.2 5.9 %copy-start.3 = (bf16[128,3072]{1,0:T(8,128)(2,1)S(1)}, bf16[128,3072]{1,0:T(8,128)(2,1)}, u32[]{:S(2)}) copy-start(bf16[128,3072]{1,0:T(8,128)(2,1)} %param.12) | copy-start | bytes 2359300
  59.2 164.9 %all-gather.5.cloned.1.call-start = ((), (), s32[]{:S(2)}) async-start(), calls=%async_computation.4 | async-start | bytes 2162688 | tf_op jit(solution)/shard_map/all_gather | solution.py:93
  61.1 8.5 %copy-start.18 = (s32[3,1]{0,1:T(1,128)S(1)}, s32[3,1]{0,1:T(1,128)}, u32[]{:S(2)}) copy-start(s32[3,1]{0,1:T(1,128)} %constant.143) | copy-start | bytes 40
  61.1 8.6 %copy-start.10 = (f32[3,128,16]{1,2,0:T(8,128)S(1)}, f32[3,128,16]{1,2,0:T(8,128)}, u32[]{:S(2)}) copy-start(f32[3,128,16]{1,2,0:T(8,128)} %param.20) | copy-start | bytes 73732
  75.1 48.5 %copy-start.6 = (bf16[128,3072]{0,1:T(8,128)(2,1)S(1)}, bf16[128,3072]{0,1:T(8,128)(2,1)}, u32[]{:S(2)}) copy-start(bf16[128,3072]{0,1:T(8,128)(2,1)} %copy.91) | copy-start | bytes 2359300
  79.7 32.8 %collective-permute-start.5 = (bf16[128,128]{0,1:T(8,128)(2,1)S(1)}, bf16[128,128]{0,1:T(8,128)(2,1)S(1)}, u32[]{:S(2)}, u32[]{:S(2)}) collective-permute-start(bf16[128,128]{0,1:T(8,128)(2,1)S(1)} %copy.92), channel_id=1, source_target_pairs={{0,12},{4,16},{8,20},{12,24},{16,28},{20,32},{24,36},{28,40},{32,4... | collective-permute-start | bytes 98312 | tf_op jit(solution)/shard_map/ppermute | solution.py:15
  112.5 8.1 %collective-permute-start.6 = (bf16[128,128]{0,1:T(8,128)(2,1)S(1)}, bf16[128,128]{0,1:T(8,128)(2,1)S(1)}, u32[]{:S(2)}, u32[]{:S(2)}) collective-permute-start(bf16[128,128]{0,1:T(8,128)(2,1)S(1)} %copy.92), channel_id=1, source_target_pairs={{0,8},{4,12},{8,16},{12,20},{16,24},{20,28},{24,32},{28,36},{32,40... | collective-permute-start | bytes 98312 | tf_op jit(solution)/shard_map/ppermute | solution.py:15
  120.7 2.1 collective-permute-start.7
  128.1 19.6 %copy-start.16 = (pred[29]{0:T(512)(128)(4,1)S(1)}, pred[29]{0:T(512)(128)(4,1)}, u32[]{:S(2)}) copy-start(pred[29]{0:T(512)(128)(4,1)} %get-tuple-element.122) | copy-start | bytes 91
  128.1 211.2 %all-to-all-start.1 = ((bf16[32,4,64,192]{3,2,1,0:T(8,128)(2,1)}), bf16[32,4,64,192]{3,2,1,0:T(8,128)(2,1)}, u32[]{:S(2)}, u32[]{:S(2)}) async-start(bf16[32,4,64,192]{3,2,1,0:T(8,128)(2,1)} %broadcast_select_fusion), calls=%async_computation.1 | async-start | bytes 8388608 | tf_op jit(solution)/shard_map/all_to_all | solution.py:140
  229.7 5.8 %copy-start.2 = (f32[1024,2048]{1,0:T(8,128)S(1)}, f32[1024,2048]{1,0:T(8,128)}, u32[]{:S(2)}) copy-start(f32[1024,2048]{1,0:T(8,128)} %get-tuple-element.183) | copy-start | bytes 25165828 | tf_op jit(solution)/shard_map/while
  258.3 5.8 %copy-start.2 = (f32[1024,2048]{1,0:T(8,128)S(1)}, f32[1024,2048]{1,0:T(8,128)}, u32[]{:S(2)}) copy-start(f32[1024,2048]{1,0:T(8,128)} %get-tuple-element.183) | copy-start | bytes 25165828 | tf_op jit(solution)/shard_map/while
  349.5 7.0 %copy-start.1 = (bf16[4096,128]{1,0:T(8,128)(2,1)S(1)}, bf16[4096,128]{1,0:T(8,128)(2,1)}, u32[]{:S(2)}) copy-start(bf16[4096,128]{1,0:T(8,128)(2,1)} %param.16) | copy-start | bytes 3145732
  (16 other events, 57.5 us)
Sparse Core Ops, SparseCore 0:
  15.0 112.5 all-gather.2
  130.1 93.9 all-gather.4
where the time goes:
time: 365 us; the launch traced here: 363 us
  waiting for transfers between devices  102 us (28%)
  matrix products  82.9 us (23%)
  starting transfers between devices  65.1 us (18%)
  other arithmetic  57.9 us (16%)
  local copies, waits for them, and re-layouts  40.9 us (11%)
  between operations  14.1 us (4%)
    all_gather x1, waiting for transfers between devices, on_device(): piece_values = lax.all_gather(packed_values, 'ctx', axis=0, tiled=True)  69.5 us
    dot_general x8, matrix products, absorb(): lax.dot_general(query_rows, some_keys, (((1,), (1,)), ((), ())), preferre...  44.4 us
    reduce_sum x8, other arithmetic, absorb(): running_total = running_total * factor + jnp.sum(branch_weights, axis=1)  39.5 us
    ppermute x8, waiting for transfers between devices, passed_along(): lax.ppermute(value, axis, [(source, source + steps) for source in range(f...  32.7 us
    ppermute x8, starting transfers between devices, passed_along(): lax.ppermute(value, axis, [(source, source + steps) for source in range(f...  27.1 us
    dot_general x8, matrix products, absorb(): jnp.dot(branch_weights.astype(jnp.bfloat16), some_values, preferred_eleme...  23.5 us
    all_to_all x1, starting transfers between devices, on_device(): lax.all_to_all(sent_keys, 'ctx', split_axis=0, concat_axis=0, tiled=True)  17.3 us
    unnamed x51, local copies, waits for them, and re-layouts  15 us
  transfers between devices with their start and end apart: 13, of which 4 were waited for; matrix products, arithmetic and copies ran while one was open for 40% of the time, Pallas kernels for 0%

commit v1 on v0

--- a/solution.py
+++ b/solution.py
@@ -90,7 +90,11 @@
         jnp.zeros((row_count, value_width), jnp.float32),
     )
     piece_keys = lax.all_gather(packed_keys, "ctx", axis=0, tiled=True)
-    piece_values = lax.all_gather(packed_values, "ctx", axis=0, tiled=True)
+    fan = jax.lax.axis_size("ctx")
+    sides = tuple((fan if it == 0 else 1 for it in range(packed_values.ndim)))
+    piece_values = jax.lax.all_to_all(
+        jnp.tile(packed_values, sides), split_axis=0, concat_axis=0, axis_name="ctx", tiled=True
+    )
     length = piece_keys.shape[0]
     stride = math.gcd(length, 1024)
     key_block = piece_keys.reshape(length // stride, stride, key_width)

time: 365 us -> 338 us (0.926)
  waiting for transfers between devices: 102 us -> 57.7 us
  blocking collectives: 0 us -> 20.9 us
  starting transfers between devices: 65.1 us -> 56.4 us
  local copies, waits for them, and re-layouts: 40.9 us -> 45.6 us
    all_gather x1 -> x0, waiting for transfers between devices: 69.5 us -> none  [on_device(): piece_values = lax.all_gather(packed_values, 'ctx', axis=0, tiled=True)]
    all_to_all x0 -> x1, blocking collectives: none -> 20.9 us  [on_device(): lax.all_to_all(asked_here, 'ctx', split_axis=0, concat_axis=0, tiled=True)]
    all_to_all x1, waiting for transfers between devices: 0.01 us -> 20.1 us  [on_device(): lax.all_to_all(sent_values, 'ctx', split_axis=0, concat_axis=0, tiled=True)]
    all_to_all x1, starting transfers between devices: 11.3 us -> 5.55 us  [on_device(): jax.lax.all_to_all(jnp.tile(packed_values, sides), split_axis=0, concat_a...]
    ppermute x8, waiting for transfers between devices: 32.7 us -> 37.6 us  [passed_along(): lax.ppermute(value, axis, [(source, source + steps) for source in range(f...]
    all_to_all x1, starting transfers between devices: 9.34 us -> 4.77 us  [on_device(): lax.all_to_all(sent_values, 'ctx', split_axis=0, concat_axis=0, tiled=True)]
    unnamed x51 -> x49, local copies, waits for them, and re-layouts: 15 us -> 16.7 us
  transfers between devices with their start and end apart: 13 -> 12, of which waited for: 4 -> 4; matrix products, arithmetic and copies ran while one was open for 40% -> 45% of each run, Pallas kernels for 0% -> 0%
where the time goes in v1:
time: 338 us; the launch traced here: 335 us
  matrix products  82.1 us (24%)
  other arithmetic  58 us (17%)
  waiting for transfers between devices  57.7 us (17%)
  starting transfers between devices  56.4 us (17%)
  local copies, waits for them, and re-layouts  45.6 us (13%)
  blocking collectives  20.9 us (6%)
  between operations  14.1 us (4%)
    dot_general x8, matrix products, absorb(): lax.dot_general(query_rows, some_keys, (((1,), (1,)), ((), ())), preferre...  44.4 us
    reduce_sum x8, other arithmetic, absorb(): running_total = running_total * factor + jnp.sum(branch_weights, axis=1)  39.5 us
    ppermute x8, waiting for transfers between devices, passed_along(): lax.ppermute(value, axis, [(source, source + steps) for source in range(f...  37.6 us
    ppermute x8, starting transfers between devices, passed_along(): lax.ppermute(value, axis, [(source, source + steps) for source in range(f...  28.2 us
    dot_general x8, matrix products, absorb(): jnp.dot(branch_weights.astype(jnp.bfloat16), some_values, preferred_eleme...  23.5 us
    all_to_all x1, blocking collectives, on_device(): lax.all_to_all(asked_here, 'ctx', split_axis=0, concat_axis=0, tiled=True)  20.9 us
    all_to_all x1, waiting for transfers between devices, on_device(): lax.all_to_all(sent_values, 'ctx', split_axis=0, concat_axis=0, tiled=True)  20.1 us
    all_to_all x1, starting transfers between devices, on_device(): lax.all_to_all(sent_keys, 'ctx', split_axis=0, concat_axis=0, tiled=True)  17.9 us
  transfers between devices with their start and end apart: 12, of which 4 were waited for; matrix products, arithmetic and copies ran while one was open for 45% of the time, Pallas kernels for 0%

profile of v1, /device:TPU:24, one launch (start us, length us, event | category | flops | bytes accessed | tf_op | source)
XLA Modules:
  0.0 335.1 jit_solution(10130451531627202913)
XLA Ops:
  10.2 20.9 %all_to_all.25 = s32[32,1,4]{2,1,0:T(1,128)S(1)} all-to-all(s32[32,1,4]{2,1,0:T(1,128)S(1)} %bitcast.114), channel_id=1, replica_groups=mesh['ctx'=32,'pb'=2,'ga'=4] {'ctx'}, dimensions={0} | all-to-all | bytes 1024 | tf_op jit(solution)/shard_map/all_to_all | solution.py:135
  77.4 20.1 %all-to-all-done.3 = bf16[32,4,64,128]{3,2,1,0:T(8,128)(2,1)} async-done(((bf16[32,4,64,128]{3,2,1,0:T(8,128)(2,1)}), bf16[32,4,64,128]{3,2,1,0:T(8,128)(2,1)}, u32[]{:S(2)}, u32[]{:S(2)}) %all-to-all-start.3) | async-done | bytes 2097184 | tf_op jit(solution)/shard_map/all_to_all | solution.py:145
  99.3 5.6 %all-to-all-start = ((bf16[32,256,128]{2,1,0:T(8,128)(2,1)}), bf16[32,256,128]{2,1,0:T(8,128)(2,1)}, u32[]{:S(2)}, u32[]{:S(2)}) async-start(bf16[32,256,128]{2,1,0:T(8,128)(2,1)} %tile.2), calls=%async_computation | async-start | bytes 4194304 | tf_op jit(solution)/shard_map/all_to_all | solution.py:95
  116.5 35.4 %collective-permute-done.5 = bf16[128,128]{0,1:T(8,128)(2,1)S(1)} collective-permute-done((bf16[128,128]{0,1:T(8,128)(2,1)S(1)}, bf16[128,128]{0,1:T(8,128)(2,1)S(1)}, u32[]{:S(2)}, u32[]{:S(2)}) %collective-permute-start.5) | collective-permute-done | bytes 32800 | tf_op jit(solution)/shard_map/ppermute | solution.py:15
  151.8 8.0 %collective-permute-start.6 = (bf16[128,128]{0,1:T(8,128)(2,1)S(1)}, bf16[128,128]{0,1:T(8,128)(2,1)S(1)}, u32[]{:S(2)}, u32[]{:S(2)}) collective-permute-start(bf16[128,128]{0,1:T(8,128)(2,1)S(1)} %copy.92), channel_id=1, source_target_pairs={{0,8},{4,12},{8,16},{12,20},{16,24},{20,28},{24,32},{28,36},{32,40... | collective-permute-start | bytes 98312 | tf_op jit(solution)/shard_map/ppermute | solution.py:15
  172.2 6.0 %copy.102 = bf16[8192,192]{1,0:T(8,128)(2,1)} copy(bf16[8192,192]{0,1:T(8,128)(2,1)} %all-gather.2.cloned.1.call-done) | data formatting | bytes 6291456
  178.1 17.9 %all-to-all-start.2 = ((bf16[32,4,64,192]{3,2,1,0:T(8,128)(2,1)}), bf16[32,4,64,192]{3,2,1,0:T(8,128)(2,1)}, u32[]{:S(2)}, u32[]{:S(2)}) async-start(bf16[32,4,64,192]{3,2,1,0:T(8,128)(2,1)} %broadcast_select_fusion), calls=%async_computation.2 | async-start | bytes 8388608 | tf_op jit(solution)/shard_map/all_to_all | solution.py:144
  196.0 114.4 %while.15 = (s32[]{:T(128)}, f32[2048]{0:T(1024)S(1)}, f32[2048]{0:T(1024)S(1)}, f32[2048,128]{1,0:T(8,128)S(1)}, bf16[8,1024,192]{2,1,0:T(8,128)(2,1)}, /*index...) while((s32[]{:T(128)}, f32[2048]{0:T(1024)S(1)}, ...), condition=%wide.region_7.8_spmd.clone, body=%wide.region_4.7_spmd.clone.sunk | while | flops 1359751168 | bytes 62522500 | solution.py:121
  196.1 5.6 %multiply_reduce_fusion.2 = (f32[2048]{0:T(1024)S(1)}, f32[1024,2048]{1,0:T(8,128)}) fusion(bf16[2048,192]{1,0:T(8,128)(2,1)S(1)} %get-tuple-element.209, bf16[8,1024,192]{2,1,0:T(8,128)(2,1)} %get-tuple-element.208, s32[]{:T(128)} %get-tuple-element.195), kind=kOutput, calls=%fused_computation.5.clone.1 | convolution fusion | flops 809498624 | bytes 9708032 | tf_op jit(solution)/shard_map/while/body/eval_jaxpr/dot_general | solution.py:107
  201.6 4.9 %fusion.72 = f32[2048]{0:T(1024)S(1)} fusion(f32[1024,2048]{1,0:T(8,128)} %get-tuple-element.183, f32[2048]{0:T(1024)S(1)} %select_maximum_fusion.2), kind=kLoop, calls=%fused_computation.7.clone.1 | loop fusion | flops 6289408 | bytes 8404992 | tf_op jit(solution)/shard_map/while/body/eval_jaxpr/reduce_sum | solution.py:115
  210.4 5.6 %multiply_reduce_fusion.2 = (f32[2048]{0:T(1024)S(1)}, f32[1024,2048]{1,0:T(8,128)}) fusion(bf16[2048,192]{1,0:T(8,128)(2,1)S(1)} %get-tuple-element.209, bf16[8,1024,192]{2,1,0:T(8,128)(2,1)} %get-tuple-element.208, s32[]{:T(128)} %get-tuple-element.195), kind=kOutput, calls=%fused_computation.5.clone.1 | convolution fusion | flops 809498624 | bytes 9708032 | tf_op jit(solution)/shard_map/while/body/eval_jaxpr/dot_general | solution.py:107
  215.9 4.9 %fusion.72 = f32[2048]{0:T(1024)S(1)} fusion(f32[1024,2048]{1,0:T(8,128)} %get-tuple-element.183, f32[2048]{0:T(1024)S(1)} %select_maximum_fusion.2), kind=kLoop, calls=%fused_computation.7.clone.1 | loop fusion | flops 6289408 | bytes 8404992 | tf_op jit(solution)/shard_map/while/body/eval_jaxpr/reduce_sum | solution.py:115
  224.7 5.6 %multiply_reduce_fusion.2 = (f32[2048]{0:T(1024)S(1)}, f32[1024,2048]{1,0:T(8,128)}) fusion(bf16[2048,192]{1,0:T(8,128)(2,1)S(1)} %get-tuple-element.209, bf16[8,1024,192]{2,1,0:T(8,128)(2,1)} %get-tuple-element.208, s32[]{:T(128)} %get-tuple-element.195), kind=kOutput, calls=%fused_computation.5.clone.1 | convolution fusion | flops 809498624 | bytes 9708032 | tf_op jit(solution)/shard_map/while/body/eval_jaxpr/dot_general | solution.py:107
  230.2 4.9 %fusion.72 = f32[2048]{0:T(1024)S(1)} fusion(f32[1024,2048]{1,0:T(8,128)} %get-tuple-element.183, f32[2048]{0:T(1024)S(1)} %select_maximum_fusion.2), kind=kLoop, calls=%fused_computation.7.clone.1 | loop fusion | flops 6289408 | bytes 8404992 | tf_op jit(solution)/shard_map/while/body/eval_jaxpr/reduce_sum | solution.py:115
  239.0 5.6 %multiply_reduce_fusion.2 = (f32[2048]{0:T(1024)S(1)}, f32[1024,2048]{1,0:T(8,128)}) fusion(bf16[2048,192]{1,0:T(8,128)(2,1)S(1)} %get-tuple-element.209, bf16[8,1024,192]{2,1,0:T(8,128)(2,1)} %get-tuple-element.208, s32[]{:T(128)} %get-tuple-element.195), kind=kOutput, calls=%fused_computation.5.clone.1 | convolution fusion | flops 809498624 | bytes 9708032 | tf_op jit(solution)/shard_map/while/body/eval_jaxpr/dot_general | solution.py:107
  244.5 4.9 %fusion.72 = f32[2048]{0:T(1024)S(1)} fusion(f32[1024,2048]{1,0:T(8,128)} %get-tuple-element.183, f32[2048]{0:T(1024)S(1)} %select_maximum_fusion.2), kind=kLoop, calls=%fused_computation.7.clone.1 | loop fusion | flops 6289408 | bytes 8404992 | tf_op jit(solution)/shard_map/while/body/eval_jaxpr/reduce_sum | solution.py:115
  253.3 5.6 %multiply_reduce_fusion.2 = (f32[2048]{0:T(1024)S(1)}, f32[1024,2048]{1,0:T(8,128)}) fusion(bf16[2048,192]{1,0:T(8,128)(2,1)S(1)} %get-tuple-element.209, bf16[8,1024,192]{2,1,0:T(8,128)(2,1)} %get-tuple-element.208, s32[]{:T(128)} %get-tuple-element.195), kind=kOutput, calls=%fused_computation.5.clone.1 | convolution fusion | flops 809498624 | bytes 9708032 | tf_op jit(solution)/shard_map/while/body/eval_jaxpr/dot_general | solution.py:107
  258.8 4.9 %fusion.72 = f32[2048]{0:T(1024)S(1)} fusion(f32[1024,2048]{1,0:T(8,128)} %get-tuple-element.183, f32[2048]{0:T(1024)S(1)} %select_maximum_fusion.2), kind=kLoop, calls=%fused_computation.7.clone.1 | loop fusion | flops 6289408 | bytes 8404992 | tf_op jit(solution)/shard_map/while/body/eval_jaxpr/reduce_sum | solution.py:115
  267.6 5.6 %multiply_reduce_fusion.2 = (f32[2048]{0:T(1024)S(1)}, f32[1024,2048]{1,0:T(8,128)}) fusion(bf16[2048,192]{1,0:T(8,128)(2,1)S(1)} %get-tuple-element.209, bf16[8,1024,192]{2,1,0:T(8,128)(2,1)} %get-tuple-element.208, s32[]{:T(128)} %get-tuple-element.195), kind=kOutput, calls=%fused_computation.5.clone.1 | convolution fusion | flops 809498624 | bytes 9708032 | tf_op jit(solution)/shard_map/while/body/eval_jaxpr/dot_general | solution.py:107
  273.1 4.9 %fusion.72 = f32[2048]{0:T(1024)S(1)} fusion(f32[1024,2048]{1,0:T(8,128)} %get-tuple-element.183, f32[2048]{0:T(1024)S(1)} %select_maximum_fusion.2), kind=kLoop, calls=%fused_computation.7.clone.1 | loop fusion | flops 6289408 | bytes 8404992 | tf_op jit(solution)/shard_map/while/body/eval_jaxpr/reduce_sum | solution.py:115
  281.9 5.6 %multiply_reduce_fusion.2 = (f32[2048]{0:T(1024)S(1)}, f32[1024,2048]{1,0:T(8,128)}) fusion(bf16[2048,192]{1,0:T(8,128)(2,1)S(1)} %get-tuple-element.209, bf16[8,1024,192]{2,1,0:T(8,128)(2,1)} %get-tuple-element.208, s32[]{:T(128)} %get-tuple-element.195), kind=kOutput, calls=%fused_computation.5.clone.1 | convolution fusion | flops 809498624 | bytes 9708032 | tf_op jit(solution)/shard_map/while/body/eval_jaxpr/dot_general | solution.py:107
  287.4 4.9 %fusion.72 = f32[2048]{0:T(1024)S(1)} fusion(f32[1024,2048]{1,0:T(8,128)} %get-tuple-element.183, f32[2048]{0:T(1024)S(1)} %select_maximum_fusion.2), kind=kLoop, calls=%fused_computation.7.clone.1 | loop fusion | flops 6289408 | bytes 8404992 | tf_op jit(solution)/shard_map/while/body/eval_jaxpr/reduce_sum | solution.py:115
  296.2 5.6 %multiply_reduce_fusion.2 = (f32[2048]{0:T(1024)S(1)}, f32[1024,2048]{1,0:T(8,128)}) fusion(bf16[2048,192]{1,0:T(8,128)(2,1)S(1)} %get-tuple-element.209, bf16[8,1024,192]{2,1,0:T(8,128)(2,1)} %get-tuple-element.208, s32[]{:T(128)} %get-tuple-element.195), kind=kOutput, calls=%fused_computation.5.clone.1 | convolution fusion | flops 809498624 | bytes 9708032 | tf_op jit(solution)/shard_map/while/body/eval_jaxpr/dot_general | solution.py:107
  301.7 4.9 %fusion.72 = f32[2048]{0:T(1024)S(1)} fusion(f32[1024,2048]{1,0:T(8,128)} %get-tuple-element.183, f32[2048]{0:T(1024)S(1)} %select_maximum_fusion.2), kind=kLoop, calls=%fused_computation.7.clone.1 | loop fusion | flops 6289408 | bytes 8404992 | tf_op jit(solution)/shard_map/while/body/eval_jaxpr/reduce_sum | solution.py:115
  (185 shorter events, 123.0 us)
Async XLA Ops:
  6.5 25.6 %copy-start = (bf16[4096,128]{1,0:T(8,128)(2,1)S(1)}, bf16[4096,128]{1,0:T(8,128)(2,1)}, u32[]{:S(2)}) copy-start(bf16[4096,128]{1,0:T(8,128)(2,1)} %param.16) | copy-start | bytes 3145732
  34.3 8.1 %copy-start.11 = (s32[1,256]{1,0:T(1,128)S(1)}, s32[1,256]{1,0:T(1,128)}, u32[]{:S(2)}) copy-start(s32[1,256]{1,0:T(1,128)} %param.17) | copy-start | bytes 3076
  34.3 10.1 %copy-start.17 = (f32[1,32]{1,0:T(1,128)S(1)}, f32[1,32]{1,0:T(1,128)}, u32[]{:S(2)}) copy-start(f32[1,32]{1,0:T(1,128)} %param.18) | copy-start | bytes 388
  37.5 60.0 %all-to-all-start.3 = ((bf16[32,4,64,128]{3,2,1,0:T(8,128)(2,1)}), bf16[32,4,64,128]{3,2,1,0:T(8,128)(2,1)}, u32[]{:S(2)}, u32[]{:S(2)}) async-start(bf16[32,4,64,128]{3,2,1,0:T(8,128)(2,1)} %broadcast_select_fusion.1), calls=%async_computation.3 | async-start | bytes 4194304 | tf_op jit(solution)/shard_map/all_to_all | solution.py:145
  42.3 129.9 %all-gather.2.cloned.1.call-start = ((), (), s32[]{:S(2)}) async-start(), calls=%async_computation.4 | async-start | bytes 3244032 | tf_op jit(solution)/shard_map/all_gather | solution.py:92
  44.6 17.6 %copy-start.9 = (bf16[128,128]{1,0:T(8,128)(2,1)S(1)}, bf16[128,128]{1,0:T(8,128)(2,1)}, u32[]{:S(2)}) copy-start(bf16[128,128]{1,0:T(8,128)(2,1)} %param.14) | copy-start | bytes 98308
  44.6 24.8 %copy-start.3 = (bf16[128,3072]{1,0:T(8,128)(2,1)S(1)}, bf16[128,3072]{1,0:T(8,128)(2,1)}, u32[]{:S(2)}) copy-start(bf16[128,3072]{1,0:T(8,128)(2,1)} %param.12) | copy-start | bytes 2359300
  48.0 116.3 %collective-permute-start = (bf16[128,192]{0,1:T(8,128)(2,1)S(1)}, bf16[128,192]{0,1:T(8,128)(2,1)S(1)}, u32[]{:S(2)}, u32[]{:S(2)}) collective-permute-start(bf16[128,192]{0,1:T(8,128)(2,1)S(1)} %copy-done.8), channel_id=1, source_target_pairs={{0,16},{4,20},{8,24},{12,28},{16,32},{20,36},{24,40},{28,44},{32,4... | collective-permute-start | bytes 147464 | tf_op jit(solution)/shard_map/ppermute | solution.py:15
  52.4 111.9 %collective-permute-start.1 = (bf16[128,192]{0,1:T(8,128)(2,1)S(1)}, bf16[128,192]{0,1:T(8,128)(2,1)S(1)}, u32[]{:S(2)}, u32[]{:S(2)}) collective-permute-start(bf16[128,192]{0,1:T(8,128)(2,1)S(1)} %copy-done.8), channel_id=1, source_target_pairs={{0,12},{4,16},{8,20},{12,24},{16,28},{20,32},{24,36},{28,40},{32,4... | collective-permute-start | bytes 147464 | tf_op jit(solution)/shard_map/ppermute | solution.py:15
  53.7 110.6 %collective-permute-start.2 = (bf16[128,192]{0,1:T(8,128)(2,1)S(1)}, bf16[128,192]{0,1:T(8,128)(2,1)S(1)}, u32[]{:S(2)}, u32[]{:S(2)}) collective-permute-start(bf16[128,192]{0,1:T(8,128)(2,1)S(1)} %copy-done.8), channel_id=1, source_target_pairs={{0,8},{4,12},{8,16},{12,20},{16,24},{20,28},{24,32},{28,36},{32,40... | collective-permute-start | bytes 147464 | tf_op jit(solution)/shard_map/ppermute | solution.py:15
  57.8 106.5 %collective-permute-start.3 = (bf16[128,192]{0,1:T(8,128)(2,1)S(1)}, bf16[128,192]{0,1:T(8,128)(2,1)S(1)}, u32[]{:S(2)}, u32[]{:S(2)}) collective-permute-start(bf16[128,192]{0,1:T(8,128)(2,1)S(1)} %copy-done.8), channel_id=1, source_target_pairs={{0,4},{4,8},{8,12},{12,16},{16,20},{20,24},{24,28},{28,32},{32,36}... | collective-permute-start | bytes 147464 | tf_op jit(solution)/shard_map/ppermute | solution.py:15
  62.3 13.8 %copy-start.16 = (s32[2,1,13]{2,1,0:T(1,128)S(1)}, s32[2,1,13]{2,1,0:T(1,128)}, u32[]{:S(2)}) copy-start(s32[2,1,13]{2,1,0:T(1,128)} %param.19) | copy-start | bytes 316
  62.3 52.1 %collective-permute-start.4 = (bf16[128,128]{0,1:T(8,128)(2,1)S(1)}, bf16[128,128]{0,1:T(8,128)(2,1)}, u32[]{:S(2)}, u32[]{:S(2)}) collective-permute-start(bf16[128,128]{0,1:T(8,128)(2,1)S(1)} %copy.92), channel_id=1, source_target_pairs={{0,16},{4,20},{8,24},{12,28},{16,32},{20,36},{24,40},{28,44},{32,4... | collective-permute-start | bytes 98312 | tf_op jit(solution)/shard_map/ppermute | solution.py:15
  77.4 27.5 %copy-start.18 = (s32[3,1]{0,1:T(1,128)S(1)}, s32[3,1]{0,1:T(1,128)}, u32[]{:S(2)}) copy-start(s32[3,1]{0,1:T(1,128)} %constant.143) | copy-start | bytes 40
  77.4 27.6 %copy-start.10 = (f32[3,128,16]{1,2,0:T(8,128)S(1)}, f32[3,128,16]{1,2,0:T(8,128)}, u32[]{:S(2)}) copy-start(f32[3,128,16]{1,2,0:T(8,128)} %param.20) | copy-start | bytes 73732
  99.3 78.8 %all-to-all-start = ((bf16[32,256,128]{2,1,0:T(8,128)(2,1)}), bf16[32,256,128]{2,1,0:T(8,128)(2,1)}, u32[]{:S(2)}, u32[]{:S(2)}) async-start(bf16[32,256,128]{2,1,0:T(8,128)(2,1)} %tile.2), calls=%async_computation | async-start | bytes 4194304 | tf_op jit(solution)/shard_map/all_to_all | solution.py:95
  109.8 54.7 %copy-start.6 = (bf16[128,3072]{0,1:T(8,128)(2,1)S(1)}, bf16[128,3072]{0,1:T(8,128)(2,1)}, u32[]{:S(2)}) copy-start(bf16[128,3072]{0,1:T(8,128)(2,1)} %copy.91) | copy-start | bytes 2359300
  114.4 37.4 %collective-permute-start.5 = (bf16[128,128]{0,1:T(8,128)(2,1)S(1)}, bf16[128,128]{0,1:T(8,128)(2,1)S(1)}, u32[]{:S(2)}, u32[]{:S(2)}) collective-permute-start(bf16[128,128]{0,1:T(8,128)(2,1)S(1)} %copy.92), channel_id=1, source_target_pairs={{0,12},{4,16},{8,20},{12,24},{16,28},{20,32},{24,36},{28,40},{32,4... | collective-permute-start | bytes 98312 | tf_op jit(solution)/shard_map/ppermute | solution.py:15
  151.8 9.6 %collective-permute-start.6 = (bf16[128,128]{0,1:T(8,128)(2,1)S(1)}, bf16[128,128]{0,1:T(8,128)(2,1)S(1)}, u32[]{:S(2)}, u32[]{:S(2)}) collective-permute-start(bf16[128,128]{0,1:T(8,128)(2,1)S(1)} %copy.92), channel_id=1, source_target_pairs={{0,8},{4,12},{8,16},{12,20},{16,24},{20,28},{24,32},{28,36},{32,40... | collective-permute-start | bytes 98312 | tf_op jit(solution)/shard_map/ppermute | solution.py:15
  161.5 2.1 collective-permute-start.7
  178.1 133.1 %all-to-all-start.2 = ((bf16[32,4,64,192]{3,2,1,0:T(8,128)(2,1)}), bf16[32,4,64,192]{3,2,1,0:T(8,128)(2,1)}, u32[]{:S(2)}, u32[]{:S(2)}) async-start(bf16[32,4,64,192]{3,2,1,0:T(8,128)(2,1)} %broadcast_select_fusion), calls=%async_computation.2 | async-start | bytes 8388608 | tf_op jit(solution)/shard_map/all_to_all | solution.py:144
  230.2 5.8 %copy-start.2 = (f32[1024,2048]{1,0:T(8,128)S(1)}, f32[1024,2048]{1,0:T(8,128)}, u32[]{:S(2)}) copy-start(f32[1024,2048]{1,0:T(8,128)} %get-tuple-element.183) | copy-start | bytes 25165828 | tf_op jit(solution)/shard_map/while
  244.5 5.8 %copy-start.2 = (f32[1024,2048]{1,0:T(8,128)S(1)}, f32[1024,2048]{1,0:T(8,128)}, u32[]{:S(2)}) copy-start(f32[1024,2048]{1,0:T(8,128)} %get-tuple-element.183) | copy-start | bytes 25165828 | tf_op jit(solution)/shard_map/while
  321.2 7.0 %copy-start.1 = (bf16[4096,128]{1,0:T(8,128)(2,1)S(1)}, bf16[4096,128]{1,0:T(8,128)(2,1)}, u32[]{:S(2)}) copy-start(bf16[4096,128]{1,0:T(8,128)(2,1)} %param.16) | copy-start | bytes 3145732
  (14 other events, 58.7 us)
Sparse Core Ops, SparseCore 0:
  48.1 118.3 all-gather.1
